TPU v7x, 32 devices: a whole 2x2x4 slice. The times are simulated.
32 devices in a mesh: grp: 4 (over x, core), dev: 8 (over z, y).
Axes of the slice: x: 2, y: 2, z: 4, core: 2. Of those that a mesh axis runs over, the one named last changes fastest.
Arguments:
- fields: float32 [24, 64, 128, 128], P(None, ('grp', 'dev')), may hold values from -6 to 6
- mix_matrix: float32 [24, 24], replicated, may hold values from -1.25 to 1.25
- laplace_matrix: float32 [24, 24], replicated, may hold values from -0.21875 to 0.21875
Outputs:
- rhs: float32 [24, 64, 128, 128], P(None, ('grp', 'dev'))
- weyl: float32 [2, 64, 128, 128], P(None, 'grp', 'dev')
All inputs are finite; a program needn't handle non-finite values.
Results may differ from a plain program's by a relative error of at most 0.0003.
Values sent between devices are 32-bit elements; how exact they have to be, the bound alone decides.
A program may use at most 192 MiB of HBM per device.

v0:
```python
import functools

import jax
import jax.numpy as jnp
from jax import lax
from jax.experimental import pallas as pl
from jax.experimental.pallas import tpu as pltpu
from jax.sharding import PartitionSpec as P

AHEAD = 24
LAG = 4
WEYL_STEPS = 4
TABLE = ((0, 1, 2), (1, 3, 4), (2, 4, 5))
PAIRS = ((0, 0), (0, 1), (0, 2), (1, 1), (1, 2), (2, 2))


def contract(tensor, left, right):
    total = None
    for first in range(3):
        for second in range(3):
            if left[first] is None or right[second] is None:
                continue
            term = tensor[TABLE[first][second]] * (left[first] * right[second])
            total = term if total is None else total + term
    return total


def weyl_pair(curv, lap, grad, along_x, along_y, along_z):
    trace = curv[0] + curv[3] + curv[5]
    electric = []
    for first, second in PAIRS:
        spot = TABLE[first][second]
        value = -0.5 * lap[spot] - trace * curv[spot]
        for middle in range(3):
            value = value + curv[TABLE[first][middle]] * curv[TABLE[middle][second]]
        electric.append(value)

    def curl(first, second):
        one = (first + 1) % 3
        two = (first + 2) % 3
        return grad[one][TABLE[two][second]] - grad[two][TABLE[one][second]]

    magnetic = [0.5 * (curl(first, second) + curl(second, first)) for first, second in PAIRS]
    square = along_x * along_x + along_y * along_y
    cylinder = jnp.sqrt(square)
    radius = jnp.sqrt(square + along_z * along_z)
    over_cyl = 1.0 / cylinder
    over_rad = 1.0 / radius
    slope = along_z * over_rad * over_cyl
    theta = (slope * along_x, slope * along_y, -cylinder * over_rad)
    phi = (-along_y * over_cyl, along_x * over_cyl, None)
    real = 0.5 * (contract(electric, theta, theta) - contract(electric, phi, phi)) - contract(
        magnetic, theta, phi
    )
    imag = -contract(electric, theta, phi) - 0.5 * (
        contract(magnetic, theta, theta) - contract(magnetic, phi, phi)
    )
    return real, imag


def kernel(
    groups,
    members,
    fields_ref,
    mix_hbm,
    lap_hbm,
    rhs_ref,
    weyl_ref,
    own,
    halo,
    lapbuf,
    laph,
    gradk,
    wtmp,
    wloc,
    wrecv,
    mix_ref,
    lap_ref,
    own_sem,
    mat_sem,
    send_p,
    recv_p,
    send_r,
    recv_r,
    send_w,
    recv_w,
):
    count, depth, rows, width = own.shape
    slabs = groups * members
    grp = lax.axis_index("grp")
    dev = lax.axis_index("dev")
    slab = grp * members + dev
    side = lax.rem(slab, 2)
    partner = slab + 1 - 2 * side
    follow = lax.rem(slab + slabs + 2 - 4 * side, slabs)
    other = lax.rem(slab + slabs - 2 + 4 * side, slabs)
    per = rows // members

    def place(index):
        return (index // members, lax.rem(index, members))

    load = pltpu.make_async_copy(fields_ref, own, own_sem)
    load.start()
    small = (
        pltpu.make_async_copy(mix_hbm, mix_ref, mat_sem.at[0]),
        pltpu.make_async_copy(lap_hbm, lap_ref, mat_sem.at[1]),
    )
    for copy in small:
        copy.start()

    def peer(offset):
        return lax.rem(dev + offset, members)

    barrier = pltpu.get_barrier_semaphore()
    for target in (follow, other):
        pl.semaphore_signal(
            barrier, inc=1, device_id=place(target), device_id_type=pl.DeviceIdType.MESH
        )
    for offset in range(1, members):
        pl.semaphore_signal(
            barrier, inc=1, device_id=(grp, peer(offset)), device_id_type=pl.DeviceIdType.MESH
        )
    pl.semaphore_wait(barrier, members + 1)

    def exchange(i, slot):
        return pltpu.make_async_remote_copy(
            src_ref=fields_ref.at[i // depth, lax.rem(i, depth)],
            dst_ref=halo.at[slot, i // depth, lax.rem(i, depth)],
            send_sem=send_p.at[i],
            recv_sem=recv_p.at[i],
            device_id=place(partner),
            device_id_type=pl.DeviceIdType.MESH,
        )

    def relay(i, slot):
        return pltpu.make_async_remote_copy(
            src_ref=halo.at[1 - side, i // depth, lax.rem(i, depth)],
            dst_ref=halo.at[slot, i // depth, lax.rem(i, depth)],
            send_sem=send_r.at[i],
            recv_sem=recv_r.at[i],
            device_id=place(follow),
            device_id_type=pl.DeviceIdType.MESH,
        )

    def spread(target, source):
        return pltpu.make_async_remote_copy(
            src_ref=wloc.at[target],
            dst_ref=wrecv.at[source],
            send_sem=send_w.at[target],
            recv_sem=recv_w.at[source],
            device_id=(grp, target),
            device_id_type=pl.DeviceIdType.MESH,
        )

    chunks = count * depth
    ahead = min(AHEAD, chunks)

    @pl.loop(0, ahead)
    def _(i):
        exchange(i, side).start()

    rhs_ref[...] = jnp.zeros_like(rhs_ref)
    load.wait()
    for copy in small:
        copy.wait()

    def advance(i):
        exchange(i, 1 - side).wait_recv()
        relay(i, side).start()

        @pl.when(i + ahead < chunks)
        def _():
            exchange(i + ahead, side).start()

    @pl.loop(0, LAG * depth)
    def _(i):
        advance(i)

    def weyl_local(part):
        tiles = rows // 8
        share = depth * tiles // WEYL_STEPS

        @pl.loop(0, share)
        def _(u):
            t = part * share + u
            p = t // tiles
            start = pl.multiple_of(lax.rem(t, tiles) * 8, 8)
            strip = pl.ds(start, 8)
            curv = [own[6 + n, p, strip, :] for n in range(6)]
            lap = [laph[n, p, strip, :] for n in range(6)]
            grad = [[gradk[n, a, p, strip, :] for n in range(6)] for a in range(3)]
            lane = lax.broadcasted_iota(jnp.int32, (8, width), 1)
            row = lax.broadcasted_iota(jnp.int32, (8, width), 0) + start
            layer = jnp.full((8, width), slab * depth + p, jnp.int32)
            along_x = lane.astype(jnp.float32) + (0.5 - 0.5 * width)
            along_y = row.astype(jnp.float32) + (0.5 - 0.5 * rows)
            along_z = layer.astype(jnp.float32) + (0.5 - 0.5 * depth * slabs)
            real, imag = weyl_pair(curv, lap, grad, along_x, along_y, along_z)
            wtmp[0, p, strip, :] = real
            wtmp[1, p, strip, :] = imag

    def process(g):
        for p in range(depth):
            f = own[g, p]
            planes = [halo[0, g, 0], halo[0, g, 1], own[g, 0], own[g, 1], halo[1, g, 0], halo[1, g, 1]]
            zm2, zm1, _, zp1, zp2 = planes[p : p + 5]
            ym1, ym2 = pltpu.roll(f, 1, 0), pltpu.roll(f, 2, 0)
            yp1, yp2 = pltpu.roll(f, rows - 1, 0), pltpu.roll(f, rows - 2, 0)
            xm1, xm2 = pltpu.roll(f, 1, 1), pltpu.roll(f, 2, 1)
            xp1, xp2 = pltpu.roll(f, width - 1, 1), pltpu.roll(f, width - 2, 1)
            near = ((zm1 + zp1) + (ym1 + yp1)) + (xm1 + xp1)
            far = ((zm2 + zp2) + (ym2 + yp2)) + (xm2 + xp2)
            lap = (16.0 * near - far - 90.0 * f) * (1.0 / 12.0)
            lapbuf[p] = lap
            gz = (8.0 * (zp1 - zm1) - (zp2 - zm2)) * (1.0 / 12.0)
            gy = (8.0 * (yp1 - ym1) - (yp2 - ym2)) * (1.0 / 12.0)
            gx = (8.0 * (xp1 - xm1) - (xp2 - xm2)) * (1.0 / 12.0)
            rhs_ref[g, p] += own[12, p] * gz + own[13, p] * gy + own[14, p] * gx

            @pl.when(g < 6)
            def _():
                laph[g, p] = lap

            @pl.when(jnp.logical_and(g >= 6, g < 12))
            def _():
                gradk[g - 6, 0, p] = gx
                gradk[g - 6, 1, p] = gy
                gradk[g - 6, 2, p] = gz

        step = 32

        @pl.loop(0, depth * (rows // step))
        def _(t):
            p = t // (rows // step)
            strip = pl.ds(pl.multiple_of(lax.rem(t, rows // step) * step, step), step)
            f = own[g, p, strip, :]
            lap = lapbuf[p, strip, :]
            for c in range(count):
                rhs_ref[c, p, strip, :] += mix_ref[c, g] * f + lap_ref[c, g] * lap

    @pl.loop(0, count)
    def _(g):
        @pl.when(g + LAG < count)
        def _():
            for p in range(depth):
                advance((g + LAG) * depth + p)

        for p in range(depth):
            relay(g * depth + p, side).wait_recv()
        process(g)

        @pl.when(jnp.logical_and(g >= 11, g < 11 + WEYL_STEPS))
        def _():
            weyl_local(g - 11)

        @pl.when(g == 11 + WEYL_STEPS)
        def _():
            for m in range(members):
                wloc[m] = wtmp[:, :, m * per : (m + 1) * per, :]

        @pl.when(g == count - LAG)
        def _():
            for offset in range(1, members):
                spread(peer(offset), dev).start()

    def put(source, block):
        for comp in range(2):
            for p in range(depth):
                weyl_ref[comp, source * depth + p] = block[comp, p]

    put(dev, wloc.at[dev])
    for offset in range(1, members):
        source = peer(offset)
        spread(source, source).wait_recv()
        put(source, wrecv.at[source])
    for offset in range(1, members):
        spread(peer(offset), dev).wait_send()

    @pl.loop(0, chunks)
    def _(i):
        exchange(i, side).wait_send()
        relay(i, side).wait_send()


def per_device(groups, members, fields, mix_matrix, laplace_matrix):
    count, depth, rows, width = fields.shape
    assert depth == 2 and (groups * members) % 2 == 0 and members % 2 == 0
    plane = (rows, width)
    per = rows // members
    vmem = functools.partial(pltpu.VMEM, dtype=jnp.float32)
    dma = pltpu.SemaphoreType.DMA
    return pl.pallas_call(
        functools.partial(kernel, groups, members),
        out_shape=(
            jax.ShapeDtypeStruct(fields.shape, jnp.float32),
            jax.ShapeDtypeStruct((2, depth * members, per, width), jnp.float32),
        ),
        in_specs=[
            pl.BlockSpec(memory_space=pltpu.HBM),
            pl.BlockSpec(memory_space=pltpu.HBM),
            pl.BlockSpec(memory_space=pltpu.HBM),
        ],
        out_specs=(
            pl.BlockSpec(memory_space=pltpu.VMEM),
            pl.BlockSpec(memory_space=pltpu.VMEM),
        ),
        scratch_shapes=[
            vmem((count, depth) + plane),
            vmem((2, count, depth) + plane),
            vmem((depth,) + plane),
            vmem((6, depth) + plane),
            vmem((6, 3, depth) + plane),
            vmem((2, depth) + plane),
            vmem((members, 2, depth, per, width)),
            vmem((members, 2, depth, per, width)),
            pltpu.SMEM((count, count), jnp.float32),
            pltpu.SMEM((count, count), jnp.float32),
            dma,
            dma((2,)),
            dma((count * depth,)),
            dma((count * depth,)),
            dma((count * depth,)),
            dma((count * depth,)),
            dma((members,)),
            dma((members,)),
        ],
        compiler_params=pltpu.CompilerParams(
            collective_id=0, has_side_effects=True, vmem_limit_bytes=48 * 1024 * 1024
        ),
        name="evolve",
    )(
        fields,
        pltpu.with_memory_space_constraint(mix_matrix, pltpu.HBM),
        pltpu.with_memory_space_constraint(laplace_matrix, pltpu.HBM),
    )


def solution(mesh):
    groups, members = mesh.shape["grp"], mesh.shape["dev"]
    return jax.shard_map(
        functools.partial(per_device, groups, members),
        mesh=mesh,
        in_specs=(P(None, ("grp", "dev"), None, None), P(), P()),
        out_specs=(P(None, ("grp", "dev"), None, None), P(None, "grp", "dev", None)),
        check_vma=False,
    )
```

profile of v0, /device:TPU:0, one launch (start us, length us, event | category | flops | bytes accessed | tf_op | source)
XLA Modules:
  0.0 88.6 jit_solution(13319044928799459197)
XLA Ops:
  0.6 85.6 %evolve.1 = (f32[24,2,128,128]{3,2,1,0:T(8,128)S(1)}, f32[2,16,16,128]{3,2,1,0:T(8,128)S(1)}) custom-call(f32[24,2,128,128]{3,2,1,0:T(8,128)} %fields_ref.1, f32[24,24]{1,0:T(8,128)} %mix_hbm.1, f32[24,24]{1,0:T(8,128)} %lap_hbm.1), custom_call_target="tpu_custom_call" | custom-call | tf_op jit(solution)/shard_map/evolve/pallas_call | solution.py:292
  86.2 1.7 %copy.7 = f32[24,2,128,128]{3,2,1,0:T(8,128)} copy(f32[24,2,128,128]{3,2,1,0:T(8,128)S(1)} %get-tuple-element.4) | data formatting | bytes 6291456
  87.9 0.7 copy.8
where the time goes:
time: 88.7 us; the launch traced here: 88.6 us
  Pallas kernels  85.6 us (97%)
  local copies, waits for them, and re-layouts  2.37 us (3%)
    pallas_call x1, Pallas kernels, per_device(): pl.pallas_call(functools.partial(kernel, groups, members), out_shape=(jax...  85.6 us
    unnamed x2, local copies, waits for them, and re-layouts  2.37 us

commit v1 on v0

--- a/solution.py
+++ b/solution.py
@@ -7,7 +7,7 @@
 from jax.experimental.pallas import tpu as pltpu
 from jax.sharding import PartitionSpec as P
 
-AHEAD = 24
+AHEAD = 6
 LAG = 4
 WEYL_STEPS = 4
 TABLE = ((0, 1, 2), (1, 3, 4), (2, 4, 5))
@@ -82,8 +82,12 @@
     recv_p,
     send_r,
     recv_r,
+    send_e,
     send_w,
     recv_w,
+    chain_sem,
+    wrap_sem,
+    ready_sem,
 ):
     count, depth, rows, width = own.shape
     slabs = groups * members
@@ -91,90 +95,164 @@
     dev = lax.axis_index("dev")
     slab = grp * members + dev
     side = lax.rem(slab, 2)
+    step = 2 - 4 * side
     partner = slab + 1 - 2 * side
-    follow = lax.rem(slab + slabs + 2 - 4 * side, slabs)
-    other = lax.rem(slab + slabs - 2 + 4 * side, slabs)
+    follow = lax.rem(slab + slabs + step, slabs)
+    far = lax.rem(slab + slabs - 1 + 2 * side, slabs)
     per = rows // members
+    first = jnp.where(side == 0, dev < 2, dev >= members - 2)
+    last = jnp.where(side == 0, dev >= members - 2, dev < 2)
+    ahead_grp = lax.rem(grp + groups + 1 - 2 * side, groups)
+    behind_grp = lax.rem(grp + groups - 1 + 2 * side, groups)
+    middle = (dev == 0) | (dev == members // 2 - 1) | (dev == members // 2) | (dev == members - 1)
 
     def place(index):
         return (index // members, lax.rem(index, members))
 
+    def signal(semaphore, target):
+        pl.semaphore_signal(
+            semaphore, inc=1, device_id=target, device_id_type=pl.DeviceIdType.MESH
+        )
+
+    barrier = pltpu.get_barrier_semaphore()
+    signal(barrier, place(partner))
+
+    @pl.when(jnp.logical_not(last))
+    def _():
+        signal(barrier, (grp, dev + step))
+
+    @pl.when(jnp.logical_not(first))
+    def _():
+        signal(barrier, (grp, dev - step))
+
+    @pl.when(last)
+    def _():
+        signal(barrier, (ahead_grp, dev))
+
     load = pltpu.make_async_copy(fields_ref, own, own_sem)
-    load.start()
     small = (
         pltpu.make_async_copy(mix_hbm, mix_ref, mat_sem.at[0]),
         pltpu.make_async_copy(lap_hbm, lap_ref, mat_sem.at[1]),
     )
-    for copy in small:
-        copy.start()
+
+    def remote(source, target, send, recv, device):
+        return pltpu.make_async_remote_copy(
+            src_ref=source,
+            dst_ref=target,
+            send_sem=send,
+            recv_sem=recv,
+            device_id=device,
+            device_id_type=pl.DeviceIdType.MESH,
+        )
 
     def peer(offset):
         return lax.rem(dev + offset, members)
 
-    barrier = pltpu.get_barrier_semaphore()
-    for target in (follow, other):
-        pl.semaphore_signal(
-            barrier, inc=1, device_id=place(target), device_id_type=pl.DeviceIdType.MESH
+    chunks = count * depth
+    final = count - 1
+    ahead = min(AHEAD, chunks)
+    ring = 2 * ahead
+
+    def exchange(i, slot):
+        g, p = i // depth, lax.rem(i, depth)
+        return remote(
+            fields_ref.at[g, p], halo.at[slot, g, p], send_p, recv_p.at[lax.rem(i, ring)], place(partner)
         )
-    for offset in range(1, members):
-        pl.semaphore_signal(
-            barrier, inc=1, device_id=(grp, peer(offset)), device_id_type=pl.DeviceIdType.MESH
-        )
-    pl.semaphore_wait(barrier, members + 1)
-
-    def exchange(i, slot):
-        return pltpu.make_async_remote_copy(
-            src_ref=fields_ref.at[i // depth, lax.rem(i, depth)],
-            dst_ref=halo.at[slot, i // depth, lax.rem(i, depth)],
-            send_sem=send_p.at[i],
-            recv_sem=recv_p.at[i],
-            device_id=place(partner),
-            device_id_type=pl.DeviceIdType.MESH,
-        )
-
-    def relay(i, slot):
-        return pltpu.make_async_remote_copy(
-            src_ref=halo.at[1 - side, i // depth, lax.rem(i, depth)],
-            dst_ref=halo.at[slot, i // depth, lax.rem(i, depth)],
-            send_sem=send_r.at[i],
-            recv_sem=recv_r.at[i],
-            device_id=place(follow),
-            device_id_type=pl.DeviceIdType.MESH,
-        )
+
+    def relay(g, p, slot, send):
+        recv = recv_r.at[g] if p is None or not isinstance(g, int) else recv_r.at[g + p]
+        return remote(halo.at[1 - side, g, p], halo.at[slot, g, p], send, recv, place(follow))
+
+    direct = remote(
+        fields_ref.at[final, depth - 1],
+        halo.at[1 - side, final, depth - 1],
+        send_e.at[2],
+        recv_r.at[final + 1],
+        place(far),
+    )
 
     def spread(target, source):
-        return pltpu.make_async_remote_copy(
-            src_ref=wloc.at[target],
-            dst_ref=wrecv.at[source],
-            send_sem=send_w.at[target],
-            recv_sem=recv_w.at[source],
-            device_id=(grp, target),
-            device_id_type=pl.DeviceIdType.MESH,
-        )
-
-    chunks = count * depth
-    ahead = min(AHEAD, chunks)
+        return remote(wloc.at[target], wrecv.at[source], send_w, recv_w, (grp, target))
+
+    pl.semaphore_wait(barrier, jnp.where(first, 2, 3))
 
     @pl.loop(0, ahead)
     def _(i):
         exchange(i, side).start()
+
+    load.start()
+    for copy in small:
+        copy.start()
+
+    @pl.when(jnp.logical_not(last))
+    def _():
+        signal(ready_sem, place(partner))
+
+    @pl.when(first)
+    def _():
+        signal(chain_sem, (grp, dev + step))
+
+    @pl.when(jnp.logical_not(first))
+    def _():
+        pl.semaphore_wait(chain_sem, 1)
+
+        @pl.when(last)
+        def _():
+            signal(wrap_sem, (behind_grp, dev))
+
+        @pl.when(jnp.logical_not(last))
+        def _():
+            signal(chain_sem, (grp, dev + step))
+
+    @pl.when(last)
+    def _():
+        pl.semaphore_wait(wrap_sem, 1)
+        signal(ready_sem, place(partner))
+
+    pl.semaphore_wait(ready_sem, 1)
+
+    @pl.when(middle)
+    def _():
+        direct.start()
+
+    def advance(i):
+        exchange(i, 1 - side).wait_recv()
+        g, p = i // depth, lax.rem(i, depth)
+
+        @pl.when(g < final)
+        def _():
+            relay(g, p, side, send_r).start()
+
+        @pl.when(i == chunks - 2)
+        def _():
+            relay(final, 0, side, send_e.at[0]).start()
+
+        @pl.when((i == chunks - 1) & middle)
+        def _():
+            relay(final, 1, side, send_e.at[1]).start()
+
+        @pl.when(i + ahead < chunks)
+        def _():
+            exchange(i + ahead, side).start()
+
+    @pl.loop(0, LAG * depth)
+    def _(i):
+        advance(i)
 
     rhs_ref[...] = jnp.zeros_like(rhs_ref)
     load.wait()
     for copy in small:
         copy.wait()
 
-    def advance(i):
-        exchange(i, 1 - side).wait_recv()
-        relay(i, side).start()
-
-        @pl.when(i + ahead < chunks)
-        def _():
-            exchange(i + ahead, side).start()
-
-    @pl.loop(0, LAG * depth)
-    def _(i):
-        advance(i)
+    def relayed(g):
+        @pl.when(g < final)
+        def _():
+            remote(halo.at[side, g], halo.at[side, g], send_r, recv_r.at[g], place(follow)).wait_recv()
+
+        @pl.when(g == final)
+        def _():
+            relay(final, 0, side, send_e.at[0]).wait_recv()
+            relay(final, 1, side, send_e.at[1]).wait_recv()
 
     def weyl_local(part):
         tiles = rows // 8
@@ -199,40 +277,38 @@
             wtmp[0, p, strip, :] = real
             wtmp[1, p, strip, :] = imag
 
-    def process(g):
-        for p in range(depth):
-            f = own[g, p]
-            planes = [halo[0, g, 0], halo[0, g, 1], own[g, 0], own[g, 1], halo[1, g, 0], halo[1, g, 1]]
-            zm2, zm1, _, zp1, zp2 = planes[p : p + 5]
-            ym1, ym2 = pltpu.roll(f, 1, 0), pltpu.roll(f, 2, 0)
-            yp1, yp2 = pltpu.roll(f, rows - 1, 0), pltpu.roll(f, rows - 2, 0)
-            xm1, xm2 = pltpu.roll(f, 1, 1), pltpu.roll(f, 2, 1)
-            xp1, xp2 = pltpu.roll(f, width - 1, 1), pltpu.roll(f, width - 2, 1)
-            near = ((zm1 + zp1) + (ym1 + yp1)) + (xm1 + xp1)
-            far = ((zm2 + zp2) + (ym2 + yp2)) + (xm2 + xp2)
-            lap = (16.0 * near - far - 90.0 * f) * (1.0 / 12.0)
-            lapbuf[p] = lap
-            gz = (8.0 * (zp1 - zm1) - (zp2 - zm2)) * (1.0 / 12.0)
-            gy = (8.0 * (yp1 - ym1) - (yp2 - ym2)) * (1.0 / 12.0)
-            gx = (8.0 * (xp1 - xm1) - (xp2 - xm2)) * (1.0 / 12.0)
-            rhs_ref[g, p] += own[12, p] * gz + own[13, p] * gy + own[14, p] * gx
-
-            @pl.when(g < 6)
-            def _():
-                laph[g, p] = lap
-
-            @pl.when(jnp.logical_and(g >= 6, g < 12))
-            def _():
-                gradk[g - 6, 0, p] = gx
-                gradk[g - 6, 1, p] = gy
-                gradk[g - 6, 2, p] = gz
-
-        step = 32
-
-        @pl.loop(0, depth * (rows // step))
+    def process(g, p):
+        f = own[g, p]
+        planes = [halo[0, g, 0], halo[0, g, 1], own[g, 0], own[g, 1], halo[1, g, 0], halo[1, g, 1]]
+        zm2, zm1, _, zp1, zp2 = planes[p : p + 5]
+        ym1, ym2 = pltpu.roll(f, 1, 0), pltpu.roll(f, 2, 0)
+        yp1, yp2 = pltpu.roll(f, rows - 1, 0), pltpu.roll(f, rows - 2, 0)
+        xm1, xm2 = pltpu.roll(f, 1, 1), pltpu.roll(f, 2, 1)
+        xp1, xp2 = pltpu.roll(f, width - 1, 1), pltpu.roll(f, width - 2, 1)
+        near = ((zm1 + zp1) + (ym1 + yp1)) + (xm1 + xp1)
+        far_sum = ((zm2 + zp2) + (ym2 + yp2)) + (xm2 + xp2)
+        lap = (16.0 * near - far_sum - 90.0 * f) * (1.0 / 12.0)
+        lapbuf[p] = lap
+        gz = (8.0 * (zp1 - zm1) - (zp2 - zm2)) * (1.0 / 12.0)
+        gy = (8.0 * (yp1 - ym1) - (yp2 - ym2)) * (1.0 / 12.0)
+        gx = (8.0 * (xp1 - xm1) - (xp2 - xm2)) * (1.0 / 12.0)
+        rhs_ref[g, p] += own[12, p] * gz + own[13, p] * gy + own[14, p] * gx
+
+        @pl.when(g < 6)
+        def _():
+            laph[g, p] = lap
+
+        @pl.when(jnp.logical_and(g >= 6, g < 12))
+        def _():
+            gradk[g - 6, 0, p] = gx
+            gradk[g - 6, 1, p] = gy
+            gradk[g - 6, 2, p] = gz
+
+        size = 32
+
+        @pl.loop(0, rows // size)
         def _(t):
-            p = t // (rows // step)
-            strip = pl.ds(pl.multiple_of(lax.rem(t, rows // step) * step, step), step)
+            strip = pl.ds(pl.multiple_of(t * size, size), size)
             f = own[g, p, strip, :]
             lap = lapbuf[p, strip, :]
             for c in range(count):
@@ -240,14 +316,20 @@
 
     @pl.loop(0, count)
     def _(g):
-        @pl.when(g + LAG < count)
-        def _():
-            for p in range(depth):
-                advance((g + LAG) * depth + p)
-
-        for p in range(depth):
-            relay(g * depth + p, side).wait_recv()
-        process(g)
+        more = g + LAG < count
+
+        @pl.when(more)
+        def _():
+            advance((g + LAG) * depth)
+
+        relayed(g)
+        process(g, 0)
+
+        @pl.when(more)
+        def _():
+            advance((g + LAG) * depth + 1)
+
+        process(g, 1)
 
         @pl.when(jnp.logical_and(g >= 11, g < 11 + WEYL_STEPS))
         def _():
@@ -258,7 +340,7 @@
             for m in range(members):
                 wloc[m] = wtmp[:, :, m * per : (m + 1) * per, :]
 
-        @pl.when(g == count - LAG)
+        @pl.when(g == 12 + WEYL_STEPS)
         def _():
             for offset in range(1, members):
                 spread(peer(offset), dev).start()
@@ -268,23 +350,27 @@
             for p in range(depth):
                 weyl_ref[comp, source * depth + p] = block[comp, p]
 
+    others = pl.ds(0, members - 1)
+    remote(wrecv.at[others], wrecv.at[others], send_w, recv_w, (grp, dev)).wait_recv()
     put(dev, wloc.at[dev])
     for offset in range(1, members):
         source = peer(offset)
-        spread(source, source).wait_recv()
         put(source, wrecv.at[source])
-    for offset in range(1, members):
-        spread(peer(offset), dev).wait_send()
-
-    @pl.loop(0, chunks)
-    def _(i):
-        exchange(i, side).wait_send()
-        relay(i, side).wait_send()
+    remote(wloc.at[others], wloc.at[others], send_w, recv_w, (grp, dev)).wait_send()
+    remote(fields_ref, halo.at[0], send_p, recv_p.at[0], place(partner)).wait_send()
+    early = pl.ds(0, final)
+    remote(halo.at[0, early], halo.at[0, early], send_r, recv_r.at[0], place(follow)).wait_send()
+    relay(final, 0, side, send_e.at[0]).wait_send()
+
+    @pl.when(middle)
+    def _():
+        relay(final, 1, side, send_e.at[1]).wait_send()
+        direct.wait_send()
 
 
 def per_device(groups, members, fields, mix_matrix, laplace_matrix):
     count, depth, rows, width = fields.shape
-    assert depth == 2 and (groups * members) % 2 == 0 and members % 2 == 0
+    assert depth == 2 and members % 4 == 0
     plane = (rows, width)
     per = rows // members
     vmem = functools.partial(pltpu.VMEM, dtype=jnp.float32)
@@ -317,12 +403,16 @@
             pltpu.SMEM((count, count), jnp.float32),
             dma,
             dma((2,)),
-            dma((count * depth,)),
-            dma((count * depth,)),
-            dma((count * depth,)),
-            dma((count * depth,)),
-            dma((members,)),
-            dma((members,)),
+            dma,
+            dma((2 * min(AHEAD, count * depth),)),
+            dma,
+            dma((count + 1,)),
+            dma((3,)),
+            dma,
+            dma,
+            pltpu.SemaphoreType.REGULAR,
+            pltpu.SemaphoreType.REGULAR,
+            pltpu.SemaphoreType.REGULAR,
         ],
         compiler_params=pltpu.CompilerParams(
             collective_id=0, has_side_effects=True, vmem_limit_bytes=48 * 1024 * 1024

time: 88.7 us -> 86.1 us (0.971)
  Pallas kernels: 85.6 us -> 82.7 us
    pallas_call x1, Pallas kernels: 85.6 us -> 82.7 us  [per_device(): pl.pallas_call(functools.partial(kernel, groups, members), out_shape=(jax...]
where the time goes in v1:
time: 86.1 us; the launch traced here: 85.7 us
  Pallas kernels  82.7 us (96%)
  local copies, waits for them, and re-layouts  2.37 us (3%)
    pallas_call x1, Pallas kernels, per_device(): pl.pallas_call(functools.partial(kernel, groups, members), out_shape=(jax...  82.7 us
    unnamed x2, local copies, waits for them, and re-layouts  2.37 us

profile of v1, /device:TPU:0, one launch (start us, length us, event | category | flops | bytes accessed | tf_op | source)
XLA Modules:
  0.0 85.7 jit_solution(6462805666508312870)
XLA Ops:
  0.6 82.7 %evolve.1 = (f32[24,2,128,128]{3,2,1,0:T(8,128)S(1)}, f32[2,16,16,128]{3,2,1,0:T(8,128)S(1)}) custom-call(f32[24,2,128,128]{3,2,1,0:T(8,128)} %fields_ref.1, f32[24,24]{1,0:T(8,128)} %mix_hbm.1, f32[24,24]{1,0:T(8,128)} %lap_hbm.1), custom_call_target="tpu_custom_call" | custom-call | tf_op jit(solution)/shard_map/evolve/pallas_call | solution.py:378
  83.3 1.7 %copy.7 = f32[24,2,128,128]{3,2,1,0:T(8,128)} copy(f32[24,2,128,128]{3,2,1,0:T(8,128)S(1)} %get-tuple-element.4) | data formatting | bytes 6291456
  85.0 0.7 copy.8

commit v2 on v1

--- a/solution.py
+++ b/solution.py
@@ -7,9 +7,11 @@
 from jax.experimental.pallas import tpu as pltpu
 from jax.sharding import PartitionSpec as P
 
-AHEAD = 6
+AHEAD = 12
 LAG = 4
 WEYL_STEPS = 4
+STRIP = 32
+HALVES = 2
 TABLE = ((0, 1, 2), (1, 3, 4), (2, 4, 5))
 PAIRS = ((0, 0), (0, 1), (0, 2), (1, 1), (1, 2), (2, 2))
 
@@ -65,7 +67,9 @@
     mix_hbm,
     lap_hbm,
     rhs_ref,
-    weyl_ref,
+    wrecv,
+    tail_ref,
+    coef_ref,
     own,
     halo,
     lapbuf,
@@ -73,7 +77,6 @@
     gradk,
     wtmp,
     wloc,
-    wrecv,
     mix_ref,
     lap_ref,
     own_sem,
@@ -82,12 +85,10 @@
     recv_p,
     send_r,
     recv_r,
-    send_e,
     send_w,
     recv_w,
     chain_sem,
     wrap_sem,
-    ready_sem,
 ):
     count, depth, rows, width = own.shape
     slabs = groups * members
@@ -98,13 +99,12 @@
     step = 2 - 4 * side
     partner = slab + 1 - 2 * side
     follow = lax.rem(slab + slabs + step, slabs)
-    far = lax.rem(slab + slabs - 1 + 2 * side, slabs)
     per = rows // members
     first = jnp.where(side == 0, dev < 2, dev >= members - 2)
     last = jnp.where(side == 0, dev >= members - 2, dev < 2)
+    second = jnp.where(side == 0, dev // 2 == 1, dev // 2 == members // 2 - 2)
     ahead_grp = lax.rem(grp + groups + 1 - 2 * side, groups)
     behind_grp = lax.rem(grp + groups - 1 + 2 * side, groups)
-    middle = (dev == 0) | (dev == members // 2 - 1) | (dev == members // 2) | (dev == members - 1)
 
     def place(index):
         return (index // members, lax.rem(index, members))
@@ -148,28 +148,28 @@
     def peer(offset):
         return lax.rem(dev + offset, members)
 
-    chunks = count * depth
+    chunks = count * depth * HALVES
     final = count - 1
     ahead = min(AHEAD, chunks)
     ring = 2 * ahead
 
+    half = rows // HALVES
+
+    def split(i):
+        part = pl.ds(pl.multiple_of(lax.rem(i, HALVES) * half, half), half)
+        return i // (HALVES * depth), lax.rem(i // HALVES, depth), part
+
     def exchange(i, slot):
-        g, p = i // depth, lax.rem(i, depth)
+        g, p, part = split(i)
         return remote(
-            fields_ref.at[g, p], halo.at[slot, g, p], send_p, recv_p.at[lax.rem(i, ring)], place(partner)
+            fields_ref.at[g, p, part], halo.at[slot, g, p, part], send_p, recv_p.at[lax.rem(i, ring)], place(partner)
         )
 
-    def relay(g, p, slot, send):
-        recv = recv_r.at[g] if p is None or not isinstance(g, int) else recv_r.at[g + p]
-        return remote(halo.at[1 - side, g, p], halo.at[slot, g, p], send, recv, place(follow))
-
-    direct = remote(
-        fields_ref.at[final, depth - 1],
-        halo.at[1 - side, final, depth - 1],
-        send_e.at[2],
-        recv_r.at[final + 1],
-        place(far),
-    )
+    def relay(i, slot):
+        g, p, part = split(i)
+        return remote(
+            halo.at[1 - side, g, p, part], halo.at[slot, g, p, part], send_r, recv_r.at[g], place(follow)
+        )
 
     def spread(target, source):
         return remote(wloc.at[target], wrecv.at[source], send_w, recv_w, (grp, target))
@@ -180,62 +180,37 @@
     def _(i):
         exchange(i, side).start()
 
+    @pl.when(jnp.logical_not(first))
+    def _():
+        @pl.when(jnp.logical_not(second))
+        def _():
+            pl.semaphore_wait(chain_sem, 1)
+
+        @pl.when(last)
+        def _():
+            signal(wrap_sem, (behind_grp, dev))
+
+        @pl.when(jnp.logical_not(last))
+        def _():
+            signal(chain_sem, (grp, dev + step))
+
     load.start()
     for copy in small:
         copy.start()
 
-    @pl.when(jnp.logical_not(last))
-    def _():
-        signal(ready_sem, place(partner))
-
-    @pl.when(first)
-    def _():
-        signal(chain_sem, (grp, dev + step))
-
-    @pl.when(jnp.logical_not(first))
-    def _():
-        pl.semaphore_wait(chain_sem, 1)
-
-        @pl.when(last)
-        def _():
-            signal(wrap_sem, (behind_grp, dev))
-
-        @pl.when(jnp.logical_not(last))
-        def _():
-            signal(chain_sem, (grp, dev + step))
-
     @pl.when(last)
     def _():
         pl.semaphore_wait(wrap_sem, 1)
-        signal(ready_sem, place(partner))
-
-    pl.semaphore_wait(ready_sem, 1)
-
-    @pl.when(middle)
-    def _():
-        direct.start()
 
     def advance(i):
         exchange(i, 1 - side).wait_recv()
-        g, p = i // depth, lax.rem(i, depth)
-
-        @pl.when(g < final)
-        def _():
-            relay(g, p, side, send_r).start()
-
-        @pl.when(i == chunks - 2)
-        def _():
-            relay(final, 0, side, send_e.at[0]).start()
-
-        @pl.when((i == chunks - 1) & middle)
-        def _():
-            relay(final, 1, side, send_e.at[1]).start()
+        relay(i, side).start()
 
         @pl.when(i + ahead < chunks)
         def _():
             exchange(i + ahead, side).start()
 
-    @pl.loop(0, LAG * depth)
+    @pl.loop(0, LAG * depth * HALVES)
     def _(i):
         advance(i)
 
@@ -243,16 +218,14 @@
     load.wait()
     for copy in small:
         copy.wait()
+    for c in range(count):
+        for which, table in enumerate((mix_ref, lap_ref)):
+            coef_ref[c, which] = jnp.full((8, width), table[c, final], jnp.float32)
+    for p in range(depth):
+        tail_ref[0, p] = own[final, p]
 
     def relayed(g):
-        @pl.when(g < final)
-        def _():
-            remote(halo.at[side, g], halo.at[side, g], send_r, recv_r.at[g], place(follow)).wait_recv()
-
-        @pl.when(g == final)
-        def _():
-            relay(final, 0, side, send_e.at[0]).wait_recv()
-            relay(final, 1, side, send_e.at[1]).wait_recv()
+        remote(halo.at[side, g], halo.at[side, g], send_r, recv_r.at[g], place(follow)).wait_recv()
 
     def weyl_local(part):
         tiles = rows // 8
@@ -289,6 +262,11 @@
         far_sum = ((zm2 + zp2) + (ym2 + yp2)) + (xm2 + xp2)
         lap = (16.0 * near - far_sum - 90.0 * f) * (1.0 / 12.0)
         lapbuf[p] = lap
+
+        @pl.when(g == final)
+        def _():
+            tail_ref[1, p] = lap
+
         gz = (8.0 * (zp1 - zm1) - (zp2 - zm2)) * (1.0 / 12.0)
         gy = (8.0 * (yp1 - ym1) - (yp2 - ym2)) * (1.0 / 12.0)
         gx = (8.0 * (xp1 - xm1) - (xp2 - xm2)) * (1.0 / 12.0)
@@ -304,11 +282,9 @@
             gradk[g - 6, 1, p] = gy
             gradk[g - 6, 2, p] = gz
 
-        size = 32
-
-        @pl.loop(0, rows // size)
+        @pl.loop(0, jnp.where(g == final, 0, rows // STRIP))
         def _(t):
-            strip = pl.ds(pl.multiple_of(t * size, size), size)
+            strip = pl.ds(pl.multiple_of(t * STRIP, STRIP), STRIP)
             f = own[g, p, strip, :]
             lap = lapbuf[p, strip, :]
             for c in range(count):
@@ -320,14 +296,16 @@
 
         @pl.when(more)
         def _():
-            advance((g + LAG) * depth)
+            for k in range(HALVES):
+                advance((g + LAG) * depth * HALVES + k)
 
         relayed(g)
         process(g, 0)
 
         @pl.when(more)
         def _():
-            advance((g + LAG) * depth + 1)
+            for k in range(HALVES):
+                advance((g + LAG) * depth * HALVES + HALVES + k)
 
         process(g, 1)
 
@@ -339,33 +317,48 @@
         def _():
             for m in range(members):
                 wloc[m] = wtmp[:, :, m * per : (m + 1) * per, :]
+            wrecv[dev] = wloc[dev]
 
         @pl.when(g == 12 + WEYL_STEPS)
         def _():
             for offset in range(1, members):
                 spread(peer(offset), dev).start()
 
-    def put(source, block):
-        for comp in range(2):
-            for p in range(depth):
-                weyl_ref[comp, source * depth + p] = block[comp, p]
-
     others = pl.ds(0, members - 1)
     remote(wrecv.at[others], wrecv.at[others], send_w, recv_w, (grp, dev)).wait_recv()
-    put(dev, wloc.at[dev])
-    for offset in range(1, members):
-        source = peer(offset)
-        put(source, wrecv.at[source])
     remote(wloc.at[others], wloc.at[others], send_w, recv_w, (grp, dev)).wait_send()
-    remote(fields_ref, halo.at[0], send_p, recv_p.at[0], place(partner)).wait_send()
-    early = pl.ds(0, final)
-    remote(halo.at[0, early], halo.at[0, early], send_r, recv_r.at[0], place(follow)).wait_send()
-    relay(final, 0, side, send_e.at[0]).wait_send()
-
-    @pl.when(middle)
-    def _():
-        relay(final, 1, side, send_e.at[1]).wait_send()
-        direct.wait_send()
+    remote(own, halo.at[0], send_p, recv_p.at[0], place(partner)).wait_send()
+    remote(halo.at[0], halo.at[0], send_r, recv_r.at[0], place(follow)).wait_send()
+
+
+def finish(members, part_ref, wrecv, tail_ref, coef_ref, rhs_ref, weyl_ref, whole, rhs_sem, weyl_sem):
+    count, depth, rows, width = part_ref.shape
+    blocks = []
+    for source in range(members):
+        layers = pl.ds(source * depth, depth)
+        blocks.append(
+            pltpu.make_async_copy(wrecv.at[source], weyl_ref.at[:, layers], weyl_sem.at[source])
+        )
+    for block in blocks:
+        block.start()
+
+    @pl.loop(0, depth * (rows // STRIP))
+    def _(t):
+        p = t // (rows // STRIP)
+        start = pl.multiple_of(lax.rem(t, rows // STRIP) * STRIP, STRIP)
+        strip = pl.ds(start, STRIP)
+        f = [tail_ref[0, p, pl.ds(start + 8 * k, 8), :] for k in range(STRIP // 8)]
+        lap = [tail_ref[1, p, pl.ds(start + 8 * k, 8), :] for k in range(STRIP // 8)]
+        for c in range(count):
+            mix, spread = coef_ref[c, 0], coef_ref[c, 1]
+            for k in range(STRIP // 8):
+                part = pl.ds(start + 8 * k, 8)
+                whole[c, p, part, :] = part_ref[c, p, part, :] + (mix * f[k] + spread * lap[k])
+        pltpu.make_async_copy(whole.at[:, p, strip], rhs_ref.at[:, p, strip], rhs_sem).start()
+
+    for block in blocks:
+        block.wait()
+    pltpu.make_async_copy(whole, rhs_ref, rhs_sem).wait()
 
 
 def per_device(groups, members, fields, mix_matrix, laplace_matrix):
@@ -375,21 +368,18 @@
     per = rows // members
     vmem = functools.partial(pltpu.VMEM, dtype=jnp.float32)
     dma = pltpu.SemaphoreType.DMA
-    return pl.pallas_call(
+    in_hbm, in_vmem = pl.BlockSpec(memory_space=pltpu.HBM), pl.BlockSpec(memory_space=pltpu.VMEM)
+    share = functools.partial(jax.ShapeDtypeStruct, dtype=jnp.float32)
+    pieces = pl.pallas_call(
         functools.partial(kernel, groups, members),
         out_shape=(
-            jax.ShapeDtypeStruct(fields.shape, jnp.float32),
-            jax.ShapeDtypeStruct((2, depth * members, per, width), jnp.float32),
+            share(fields.shape),
+            share((members, 2, depth, per, width)),
+            share((2, depth) + plane),
+            share((count, 2, 8, width)),
         ),
-        in_specs=[
-            pl.BlockSpec(memory_space=pltpu.HBM),
-            pl.BlockSpec(memory_space=pltpu.HBM),
-            pl.BlockSpec(memory_space=pltpu.HBM),
-        ],
-        out_specs=(
-            pl.BlockSpec(memory_space=pltpu.VMEM),
-            pl.BlockSpec(memory_space=pltpu.VMEM),
-        ),
+        in_specs=[in_hbm] * 3,
+        out_specs=(in_vmem,) * 4,
         scratch_shapes=[
             vmem((count, depth) + plane),
             vmem((2, count, depth) + plane),
@@ -398,31 +388,37 @@
             vmem((6, 3, depth) + plane),
             vmem((2, depth) + plane),
             vmem((members, 2, depth, per, width)),
-            vmem((members, 2, depth, per, width)),
             pltpu.SMEM((count, count), jnp.float32),
             pltpu.SMEM((count, count), jnp.float32),
             dma,
             dma((2,)),
             dma,
-            dma((2 * min(AHEAD, count * depth),)),
+            dma((2 * min(AHEAD, count * depth * HALVES),)),
             dma,
-            dma((count + 1,)),
-            dma((3,)),
+            dma((count,)),
             dma,
             dma,
             pltpu.SemaphoreType.REGULAR,
             pltpu.SemaphoreType.REGULAR,
-            pltpu.SemaphoreType.REGULAR,
         ],
         compiler_params=pltpu.CompilerParams(
-            collective_id=0, has_side_effects=True, vmem_limit_bytes=48 * 1024 * 1024
+            collective_id=0, has_side_effects=True, vmem_limit_bytes=32 * 1024 * 1024
         ),
         name="evolve",
     )(
-        fields,
+        pltpu.with_memory_space_constraint(fields, pltpu.HBM),
         pltpu.with_memory_space_constraint(mix_matrix, pltpu.HBM),
         pltpu.with_memory_space_constraint(laplace_matrix, pltpu.HBM),
     )
+    return pl.pallas_call(
+        functools.partial(finish, members),
+        out_shape=(share(fields.shape), share((2, depth * members, per, width))),
+        in_specs=[in_vmem] * 4,
+        out_specs=(in_hbm,) * 2,
+        scratch_shapes=[vmem((count, depth) + plane), dma, dma((members,))],
+        compiler_params=pltpu.CompilerParams(vmem_limit_bytes=8 * 1024 * 1024),
+        name="finish",
+    )(*pieces)
 
 
 def solution(mesh):

time: 86.1 us -> 84.7 us (0.984)
  local copies, waits for them, and re-layouts: 2.37 us -> 0 us
  Pallas kernels: 82.7 us -> 83.9 us
    unnamed x2 -> x0, local copies, waits for them, and re-layouts: 2.37 us -> none
    pallas_call x1 -> x2, Pallas kernels: 82.7 us -> 83.9 us  [the longest x1 82 us: per_device(): pl.pallas_call(functools.partial(kernel, groups, members), out_shape=(sha...]
where the time goes in v2:
time: 84.7 us; the launch traced here: 84.5 us
  Pallas kernels  83.9 us (99%)
    pallas_call x1, Pallas kernels, per_device(): pl.pallas_call(functools.partial(kernel, groups, members), out_shape=(sha...  82 us
    pallas_call x1, Pallas kernels, per_device(): pl.pallas_call(functools.partial(finish, members), out_shape=(share(field...  1.82 us

profile of v2, /device:TPU:0, one launch (start us, length us, event | category | flops | bytes accessed | tf_op | source)
XLA Modules:
  0.0 84.5 jit_solution(14998258311408924423)
XLA Ops:
  0.6 82.0 %evolve.1 = (f32[24,2,128,128]{3,2,1,0:T(8,128)S(1)}, f32[8,2,2,16,128]{4,3,2,1,0:T(8,128)S(1)}, f32[2,2,128,128]{3,2,1,0:T(8,128)S(1)}, f32[24,2,8,128]{3,2,1,0:T(8,128)S(1)}) custom-call(f32[24,2,128,128]{3,2,1,0:T(8,128)} %fields_ref.1, f32[24,24]{1,0:T(8,128)} %mix_hbm.1, f32[24,24]{1,0:T(8,128)} %lap_hbm.1), custom_call_target="tpu_custom_call" | custom-call | tf_op jit(solution)/shard_map/evolve/pallas_call | solution.py:373
  82.7 1.8 %finish.1 = (f32[24,2,128,128]{3,2,1,0:T(8,128)}, f32[2,16,16,128]{3,2,1,0:T(8,128)}) custom-call(f32[24,2,128,128]{3,2,1,0:T(8,128)S(1)} %get-tuple-element.6.part_ref, f32[8,2,2,16,128]{4,3,2,1,0:T(8,128)S(1)} %get-tuple-element.7.wrecv, f32[2,2,128,128]{3,2,1,0:T(8,128)S(1)} %get-tuple-element.8.tail_ref, f32[24,2,8,128]{3,2,1,0:T(8,128)S(1)} %get-tuple-element.9.coef_ref), custom_call_target="tpu_custom_call" | custom-call | tf_op jit(solution)/shard_map/finish/pallas_call | solution.py:413

commit v3 on v2

--- a/solution.py
+++ b/solution.py
@@ -12,6 +12,10 @@
 WEYL_STEPS = 4
 STRIP = 32
 HALVES = 2
+NEAR = 2
+FAR = 1
+LEAVE = 8
+PASS = 19
 TABLE = ((0, 1, 2), (1, 3, 4), (2, 4, 5))
 PAIRS = ((0, 0), (0, 1), (0, 2), (1, 1), (1, 2), (2, 2))
 
@@ -77,6 +81,7 @@
     gradk,
     wtmp,
     wloc,
+    passing,
     mix_ref,
     lap_ref,
     own_sem,
@@ -85,12 +90,17 @@
     recv_p,
     send_r,
     recv_r,
+    send_d,
+    recv_d,
+    send_h,
     send_w,
     recv_w,
     chain_sem,
     wrap_sem,
 ):
-    count, depth, rows, width = own.shape
+    planes_all, rows, width = own.shape
+    depth = gradk.shape[2]
+    count = planes_all // depth
     slabs = groups * members
     grp = lax.axis_index("grp")
     dev = lax.axis_index("dev")
@@ -99,6 +109,7 @@
     step = 2 - 4 * side
     partner = slab + 1 - 2 * side
     follow = lax.rem(slab + slabs + step, slabs)
+    other = lax.rem(slab + slabs - step, slabs)
     per = rows // members
     first = jnp.where(side == 0, dev < 2, dev >= members - 2)
     last = jnp.where(side == 0, dev >= members - 2, dev < 2)
@@ -157,18 +168,34 @@
 
     def split(i):
         part = pl.ds(pl.multiple_of(lax.rem(i, HALVES) * half, half), half)
-        return i // (HALVES * depth), lax.rem(i // HALVES, depth), part
+        return i // HALVES, part
 
     def exchange(i, slot):
-        g, p, part = split(i)
+        q, part = split(i)
         return remote(
-            fields_ref.at[g, p, part], halo.at[slot, g, p, part], send_p, recv_p.at[lax.rem(i, ring)], place(partner)
+            fields_ref.at[q, part], halo.at[slot, q, part], send_p, recv_p.at[lax.rem(i, ring)], place(partner)
         )
 
     def relay(i, slot):
-        g, p, part = split(i)
+        q, part = split(i)
         return remote(
-            halo.at[1 - side, g, p, part], halo.at[slot, g, p, part], send_r, recv_r.at[g], place(follow)
+            halo.at[1 - side, q, part],
+            halo.at[slot, q, part],
+            send_r.at[(q >= planes_all - NEAR).astype(jnp.int32)],
+            recv_r.at[q // depth],
+            place(follow),
+        )
+
+    def detour(planes):
+        picked = pl.ds(planes_all - planes, planes)
+        return remote(
+            fields_ref.at[picked], passing.at[pl.ds(NEAR - planes, planes)], send_d, recv_d, place(other)
+        )
+
+    def hand_on(k):
+        q = planes_all - k
+        return remote(
+            passing.at[NEAR - k], halo.at[1 - side, q], send_h.at[k - 1], recv_r.at[q // depth], place(partner)
         )
 
     def spread(target, source):
@@ -182,6 +209,10 @@
 
     @pl.when(jnp.logical_not(first))
     def _():
+        detour(NEAR).start()
+
+    @pl.when(jnp.logical_not(first))
+    def _():
         @pl.when(jnp.logical_not(second))
         def _():
             pl.semaphore_wait(chain_sem, 1)
@@ -204,7 +235,11 @@
 
     def advance(i):
         exchange(i, 1 - side).wait_recv()
-        relay(i, side).start()
+        q, _ = split(i)
+
+        @pl.when((q < planes_all - NEAR) | (last & (q < planes_all - FAR)))
+        def _():
+            relay(i, side).start()
 
         @pl.when(i + ahead < chunks)
         def _():
@@ -222,10 +257,11 @@
         for which, table in enumerate((mix_ref, lap_ref)):
             coef_ref[c, which] = jnp.full((8, width), table[c, final], jnp.float32)
     for p in range(depth):
-        tail_ref[0, p] = own[final, p]
+        tail_ref[0, p] = own[final * depth + p]
 
     def relayed(g):
-        remote(halo.at[side, g], halo.at[side, g], send_r, recv_r.at[g], place(follow)).wait_recv()
+        part = pl.ds(g * depth, depth)
+        remote(halo.at[side, part], halo.at[side, part], send_r.at[0], recv_r.at[g], place(follow)).wait_recv()
 
     def weyl_local(part):
         tiles = rows // 8
@@ -237,7 +273,7 @@
             p = t // tiles
             start = pl.multiple_of(lax.rem(t, tiles) * 8, 8)
             strip = pl.ds(start, 8)
-            curv = [own[6 + n, p, strip, :] for n in range(6)]
+            curv = [own[(6 + n) * depth + p, strip, :] for n in range(6)]
             lap = [laph[n, p, strip, :] for n in range(6)]
             grad = [[gradk[n, a, p, strip, :] for n in range(6)] for a in range(3)]
             lane = lax.broadcasted_iota(jnp.int32, (8, width), 1)
@@ -251,8 +287,9 @@
             wtmp[1, p, strip, :] = imag
 
     def process(g, p):
-        f = own[g, p]
-        planes = [halo[0, g, 0], halo[0, g, 1], own[g, 0], own[g, 1], halo[1, g, 0], halo[1, g, 1]]
+        q = g * depth
+        f = own[q + p]
+        planes = [halo[0, q], halo[0, q + 1], own[q], own[q + 1], halo[1, q], halo[1, q + 1]]
         zm2, zm1, _, zp1, zp2 = planes[p : p + 5]
         ym1, ym2 = pltpu.roll(f, 1, 0), pltpu.roll(f, 2, 0)
         yp1, yp2 = pltpu.roll(f, rows - 1, 0), pltpu.roll(f, rows - 2, 0)
@@ -270,7 +307,7 @@
         gz = (8.0 * (zp1 - zm1) - (zp2 - zm2)) * (1.0 / 12.0)
         gy = (8.0 * (yp1 - ym1) - (yp2 - ym2)) * (1.0 / 12.0)
         gx = (8.0 * (xp1 - xm1) - (xp2 - xm2)) * (1.0 / 12.0)
-        rhs_ref[g, p] += own[12, p] * gz + own[13, p] * gy + own[14, p] * gx
+        rhs_ref[g, p] += own[12 * depth + p] * gz + own[13 * depth + p] * gy + own[14 * depth + p] * gx
 
         @pl.when(g < 6)
         def _():
@@ -285,7 +322,7 @@
         @pl.loop(0, jnp.where(g == final, 0, rows // STRIP))
         def _(t):
             strip = pl.ds(pl.multiple_of(t * STRIP, STRIP), STRIP)
-            f = own[g, p, strip, :]
+            f = own[q + p, strip, :]
             lap = lapbuf[p, strip, :]
             for c in range(count):
                 rhs_ref[c, p, strip, :] += mix_ref[c, g] * f + lap_ref[c, g] * lap
@@ -308,6 +345,22 @@
                 advance((g + LAG) * depth * HALVES + HALVES + k)
 
         process(g, 1)
+
+        @pl.when((g == LEAVE) & first)
+        def _():
+            detour(FAR).start()
+
+        @pl.when((g == PASS) & last)
+        def _():
+            detour(FAR).wait_recv()
+            for k in range(FAR, 0, -1):
+                hand_on(k).start()
+
+        @pl.when((g == PASS) & jnp.logical_not(last))
+        def _():
+            detour(NEAR).wait_recv()
+            for k in range(NEAR, 0, -1):
+                hand_on(k).start()
 
         @pl.when(jnp.logical_and(g >= 11, g < 11 + WEYL_STEPS))
         def _():
@@ -328,7 +381,32 @@
     remote(wrecv.at[others], wrecv.at[others], send_w, recv_w, (grp, dev)).wait_recv()
     remote(wloc.at[others], wloc.at[others], send_w, recv_w, (grp, dev)).wait_send()
     remote(own, halo.at[0], send_p, recv_p.at[0], place(partner)).wait_send()
-    remote(halo.at[0], halo.at[0], send_r, recv_r.at[0], place(follow)).wait_send()
+    def totals(planes, semaphore):
+        part = pl.ds(0, planes)
+        remote(halo.at[0, part], halo.at[0, part], semaphore, recv_r.at[0], place(follow)).wait_send()
+
+    totals(planes_all - NEAR, send_r.at[0])
+
+    @pl.when(last)
+    def _():
+        totals(NEAR - FAR, send_r.at[1])
+
+    for k in range(NEAR, 0, -1):
+        if k <= FAR:
+            hand_on(k).wait_send()
+        else:
+
+            @pl.when(jnp.logical_not(last))
+            def _():
+                hand_on(k).wait_send()
+
+    @pl.when(first)
+    def _():
+        detour(FAR).wait_send()
+
+    @pl.when(jnp.logical_not(first))
+    def _():
+        detour(NEAR).wait_send()
 
 
 def finish(members, part_ref, wrecv, tail_ref, coef_ref, rhs_ref, weyl_ref, whole, rhs_sem, weyl_sem):
@@ -381,21 +459,25 @@
         in_specs=[in_hbm] * 3,
         out_specs=(in_vmem,) * 4,
         scratch_shapes=[
-            vmem((count, depth) + plane),
-            vmem((2, count, depth) + plane),
+            vmem((count * depth,) + plane),
+            vmem((2, count * depth) + plane),
             vmem((depth,) + plane),
             vmem((6, depth) + plane),
             vmem((6, 3, depth) + plane),
             vmem((2, depth) + plane),
             vmem((members, 2, depth, per, width)),
+            vmem((NEAR,) + plane),
             pltpu.SMEM((count, count), jnp.float32),
             pltpu.SMEM((count, count), jnp.float32),
             dma,
             dma((2,)),
             dma,
             dma((2 * min(AHEAD, count * depth * HALVES),)),
+            dma((2,)),
+            dma((count,)),
             dma,
-            dma((count,)),
+            dma,
+            dma((NEAR,)),
             dma,
             dma,
             pltpu.SemaphoreType.REGULAR,
@@ -406,7 +488,7 @@
         ),
         name="evolve",
     )(
-        pltpu.with_memory_space_constraint(fields, pltpu.HBM),
+        pltpu.with_memory_space_constraint(fields.reshape((count * depth,) + plane), pltpu.HBM),
         pltpu.with_memory_space_constraint(mix_matrix, pltpu.HBM),
         pltpu.with_memory_space_constraint(laplace_matrix, pltpu.HBM),
     )

time: 84.7 us -> 84 us (level)
  Pallas kernels: 83.9 us -> 82.9 us
    pallas_call x1, Pallas kernels: 82 us -> 81.1 us  [per_device(): pl.pallas_call(functools.partial(kernel, groups, members), out_shape=(sha...]
where the time goes in v3:
time: 84 us; the launch traced here: 83.5 us
  Pallas kernels  82.9 us (99%)
    pallas_call x1, Pallas kernels, per_device(): pl.pallas_call(functools.partial(kernel, groups, members), out_shape=(sha...  81.1 us
    pallas_call x1, Pallas kernels, per_device(): pl.pallas_call(functools.partial(finish, members), out_shape=(share(field...  1.82 us

profile of v3, /device:TPU:0, one launch (start us, length us, event | category | flops | bytes accessed | tf_op | source)
XLA Modules:
  0.0 83.5 jit_solution(6283466146880343563)
XLA Ops:
  0.6 81.1 %evolve.1 = (f32[24,2,128,128]{3,2,1,0:T(8,128)S(1)}, f32[8,2,2,16,128]{4,3,2,1,0:T(8,128)S(1)}, f32[2,2,128,128]{3,2,1,0:T(8,128)S(1)}, f32[24,2,8,128]{3,2,1,0:T(8,128)S(1)}) custom-call(f32[48,128,128]{2,1,0:T(8,128)} %bitcast.1, f32[24,24]{1,0:T(8,128)} %mix_hbm.1, f32[24,24]{1,0:T(8,128)} %lap_hbm.1), custom_call_target="tpu_custom_call" | custom-call | tf_op jit(solution)/shard_map/evolve/pallas_call | solution.py:451
  81.7 1.8 %finish.1 = (f32[24,2,128,128]{3,2,1,0:T(8,128)}, f32[2,16,16,128]{3,2,1,0:T(8,128)}) custom-call(f32[24,2,128,128]{3,2,1,0:T(8,128)S(1)} %get-tuple-element.6.part_ref, f32[8,2,2,16,128]{4,3,2,1,0:T(8,128)S(1)} %get-tuple-element.7.wrecv, f32[2,2,128,128]{3,2,1,0:T(8,128)S(1)} %get-tuple-element.8.tail_ref, f32[24,2,8,128]{3,2,1,0:T(8,128)S(1)} %get-tuple-element.9.coef_ref), custom_call_target="tpu_custom_call" | custom-call | tf_op jit(solution)/shard_map/finish/pallas_call | solution.py:495

commit v4 on v3

--- a/solution.py
+++ b/solution.py
@@ -11,11 +11,13 @@
 LAG = 4
 WEYL_STEPS = 4
 STRIP = 32
+MIX = 64
+TAIL = 2
 HALVES = 2
 NEAR = 2
-FAR = 1
+FAR = 2
 LEAVE = 8
-PASS = 19
+PASS = 18
 TABLE = ((0, 1, 2), (1, 3, 4), (2, 4, 5))
 PAIRS = ((0, 0), (0, 1), (0, 2), (1, 1), (1, 2), (2, 2))
 
@@ -229,35 +231,37 @@
     for copy in small:
         copy.start()
 
-    @pl.when(last)
-    def _():
-        pl.semaphore_wait(wrap_sem, 1)
-
-    def advance(i):
-        exchange(i, 1 - side).wait_recv()
-        q, _ = split(i)
-
-        @pl.when((q < planes_all - NEAR) | (last & (q < planes_all - FAR)))
-        def _():
-            relay(i, side).start()
-
-        @pl.when(i + ahead < chunks)
-        def _():
-            exchange(i + ahead, side).start()
-
-    @pl.loop(0, LAG * depth * HALVES)
-    def _(i):
-        advance(i)
-
     rhs_ref[...] = jnp.zeros_like(rhs_ref)
     load.wait()
     for copy in small:
         copy.wait()
     for c in range(count):
-        for which, table in enumerate((mix_ref, lap_ref)):
-            coef_ref[c, which] = jnp.full((8, width), table[c, final], jnp.float32)
-    for p in range(depth):
-        tail_ref[0, p] = own[final * depth + p]
+        for k in range(TAIL):
+            coef_ref[c, k] = jnp.full((8, width), mix_ref[c, count - TAIL + k], jnp.float32)
+            coef_ref[c, TAIL + k] = jnp.full((8, width), lap_ref[c, count - TAIL + k], jnp.float32)
+    for k in range(TAIL):
+        for p in range(depth):
+            tail_ref[k, p] = own[(count - TAIL + k) * depth + p]
+
+    @pl.when(last)
+    def _():
+        pl.semaphore_wait(wrap_sem, 1)
+
+    def advance(i):
+        exchange(i, 1 - side).wait_recv()
+        q, _ = split(i)
+
+        @pl.when((q < planes_all - NEAR) | (last & (q < planes_all - FAR)))
+        def _():
+            relay(i, side).start()
+
+        @pl.when(i + ahead < chunks)
+        def _():
+            exchange(i + ahead, side).start()
+
+    @pl.loop(0, LAG * depth * HALVES)
+    def _(i):
+        advance(i)
 
     def relayed(g):
         part = pl.ds(g * depth, depth)
@@ -300,9 +304,9 @@
         lap = (16.0 * near - far_sum - 90.0 * f) * (1.0 / 12.0)
         lapbuf[p] = lap
 
-        @pl.when(g == final)
-        def _():
-            tail_ref[1, p] = lap
+        @pl.when(g >= count - TAIL)
+        def _():
+            tail_ref[g - (count - 2 * TAIL), p] = lap
 
         gz = (8.0 * (zp1 - zm1) - (zp2 - zm2)) * (1.0 / 12.0)
         gy = (8.0 * (yp1 - ym1) - (yp2 - ym2)) * (1.0 / 12.0)
@@ -319,9 +323,9 @@
             gradk[g - 6, 1, p] = gy
             gradk[g - 6, 2, p] = gz
 
-        @pl.loop(0, jnp.where(g == final, 0, rows // STRIP))
+        @pl.loop(0, jnp.where(g >= count - TAIL, 0, rows // MIX))
         def _(t):
-            strip = pl.ds(pl.multiple_of(t * STRIP, STRIP), STRIP)
+            strip = pl.ds(pl.multiple_of(t * MIX, MIX), MIX)
             f = own[q + p, strip, :]
             lap = lapbuf[p, strip, :]
             for c in range(count):
@@ -425,13 +429,17 @@
         p = t // (rows // STRIP)
         start = pl.multiple_of(lax.rem(t, rows // STRIP) * STRIP, STRIP)
         strip = pl.ds(start, STRIP)
-        f = [tail_ref[0, p, pl.ds(start + 8 * k, 8), :] for k in range(STRIP // 8)]
-        lap = [tail_ref[1, p, pl.ds(start + 8 * k, 8), :] for k in range(STRIP // 8)]
+        terms = [
+            [tail_ref[k, p, pl.ds(start + 8 * r, 8), :] for r in range(STRIP // 8)] for k in range(2 * TAIL)
+        ]
         for c in range(count):
-            mix, spread = coef_ref[c, 0], coef_ref[c, 1]
-            for k in range(STRIP // 8):
-                part = pl.ds(start + 8 * k, 8)
-                whole[c, p, part, :] = part_ref[c, p, part, :] + (mix * f[k] + spread * lap[k])
+            coefs = [coef_ref[c, k] for k in range(2 * TAIL)]
+            for r in range(STRIP // 8):
+                part = pl.ds(start + 8 * r, 8)
+                value = part_ref[c, p, part, :]
+                for k in range(2 * TAIL):
+                    value = value + coefs[k] * terms[k][r]
+                whole[c, p, part, :] = value
         pltpu.make_async_copy(whole.at[:, p, strip], rhs_ref.at[:, p, strip], rhs_sem).start()
 
     for block in blocks:
@@ -453,8 +461,8 @@
         out_shape=(
             share(fields.shape),
             share((members, 2, depth, per, width)),
-            share((2, depth) + plane),
-            share((count, 2, 8, width)),
+            share((2 * TAIL, depth) + plane),
+            share((count, 2 * TAIL, 8, width)),
         ),
         in_specs=[in_hbm] * 3,
         out_specs=(in_vmem,) * 4,

time: 84 us -> 83.5 us (level)
    pallas_call x1, Pallas kernels: 81.1 us -> 80.2 us  [per_device(): pl.pallas_call(functools.partial(kernel, groups, members), out_shape=(sha...]
where the time goes in v4:
time: 83.5 us; the launch traced here: 82.7 us
  Pallas kernels  82.1 us (98%)
    pallas_call x1, Pallas kernels, per_device(): pl.pallas_call(functools.partial(kernel, groups, members), out_shape=(sha...  80.2 us
    pallas_call x1, Pallas kernels, per_device(): pl.pallas_call(functools.partial(finish, members), out_shape=(share(field...  1.85 us

profile of v4, /device:TPU:0, one launch (start us, length us, event | category | flops | bytes accessed | tf_op | source)
XLA Modules:
  0.0 82.7 jit_solution(45137461780197)
XLA Ops:
  0.6 80.2 %evolve.1 = (f32[24,2,128,128]{3,2,1,0:T(8,128)S(1)}, f32[8,2,2,16,128]{4,3,2,1,0:T(8,128)S(1)}, f32[4,2,128,128]{3,2,1,0:T(8,128)S(1)}, f32[24,4,8,128]{3,2,1,0:T(8,128)S(1)}) custom-call(f32[48,128,128]{2,1,0:T(8,128)} %bitcast.1, f32[24,24]{1,0:T(8,128)} %mix_hbm.1, f32[24,24]{1,0:T(8,128)} %lap_hbm.1), custom_call_target="tpu_custom_call" | custom-call | tf_op jit(solution)/shard_map/evolve/pallas_call | solution.py:459
  80.9 1.9 %finish.1 = (f32[24,2,128,128]{3,2,1,0:T(8,128)}, f32[2,16,16,128]{3,2,1,0:T(8,128)}) custom-call(f32[24,2,128,128]{3,2,1,0:T(8,128)S(1)} %get-tuple-element.6.part_ref, f32[8,2,2,16,128]{4,3,2,1,0:T(8,128)S(1)} %get-tuple-element.7.wrecv, f32[4,2,128,128]{3,2,1,0:T(8,128)S(1)} %get-tuple-element.8.tail_ref, f32[24,4,8,128]{3,2,1,0:T(8,128)S(1)} %get-tuple-element.9.coef_ref), custom_call_target="tpu_custom_call" | custom-call | tf_op jit(solution)/shard_map/finish/pallas_call | solution.py:503

commit v5 on v4

--- a/solution.py
+++ b/solution.py
@@ -10,6 +10,8 @@
 AHEAD = 12
 LAG = 4
 WEYL_STEPS = 4
+SPREAD_EVEN = 16
+SPREAD_ODD = 20
 STRIP = 32
 MIX = 64
 TAIL = 2
@@ -290,10 +292,7 @@
             wtmp[0, p, strip, :] = real
             wtmp[1, p, strip, :] = imag
 
-    def process(g, p):
-        q = g * depth
-        f = own[q + p]
-        planes = [halo[0, q], halo[0, q + 1], own[q], own[q + 1], halo[1, q], halo[1, q + 1]]
+    def stencil(f, planes, p):
         zm2, zm1, _, zp1, zp2 = planes[p : p + 5]
         ym1, ym2 = pltpu.roll(f, 1, 0), pltpu.roll(f, 2, 0)
         yp1, yp2 = pltpu.roll(f, rows - 1, 0), pltpu.roll(f, rows - 2, 0)
@@ -302,15 +301,16 @@
         near = ((zm1 + zp1) + (ym1 + yp1)) + (xm1 + xp1)
         far_sum = ((zm2 + zp2) + (ym2 + yp2)) + (xm2 + xp2)
         lap = (16.0 * near - far_sum - 90.0 * f) * (1.0 / 12.0)
-        lapbuf[p] = lap
-
-        @pl.when(g >= count - TAIL)
-        def _():
-            tail_ref[g - (count - 2 * TAIL), p] = lap
-
         gz = (8.0 * (zp1 - zm1) - (zp2 - zm2)) * (1.0 / 12.0)
         gy = (8.0 * (yp1 - ym1) - (yp2 - ym2)) * (1.0 / 12.0)
         gx = (8.0 * (xp1 - xm1) - (xp2 - xm2)) * (1.0 / 12.0)
+        return lap, gx, gy, gz
+
+    def process(g, p):
+        q = g * depth
+        planes = [halo[0, q], halo[0, q + 1], own[q], own[q + 1], halo[1, q], halo[1, q + 1]]
+        lap, gx, gy, gz = stencil(own[q + p], planes, p)
+        lapbuf[p] = lap
         rhs_ref[g, p] += own[12 * depth + p] * gz + own[13 * depth + p] * gy + own[14 * depth + p] * gx
 
         @pl.when(g < 6)
@@ -323,7 +323,7 @@
             gradk[g - 6, 1, p] = gy
             gradk[g - 6, 2, p] = gz
 
-        @pl.loop(0, jnp.where(g >= count - TAIL, 0, rows // MIX))
+        @pl.loop(0, rows // MIX)
         def _(t):
             strip = pl.ds(pl.multiple_of(t * MIX, MIX), MIX)
             f = own[q + p, strip, :]
@@ -331,7 +331,43 @@
             for c in range(count):
                 rhs_ref[c, p, strip, :] += mix_ref[c, g] * f + lap_ref[c, g] * lap
 
-    @pl.loop(0, count)
+    def without_far(g, p):
+        q = g * depth
+        zero = jnp.zeros(own.shape[1:], jnp.float32)
+        for parity in range(2):
+
+            @pl.when(side == parity)
+            def _():
+                low = [zero] * depth if parity == 0 else [halo[0, q + k] for k in range(depth)]
+                high = [zero] * depth if parity == 1 else [halo[1, q + k] for k in range(depth)]
+                planes = low + [own[q + k] for k in range(depth)] + high
+                lap, gx, gy, gz = stencil(own[q + p], planes, p)
+                tail_ref[g - (count - 2 * TAIL), p] = lap
+                rhs_ref[g, p] += (
+                    own[12 * depth + p] * gz + own[13 * depth + p] * gy + own[14 * depth + p] * gx
+                )
+
+    def far_share(g, p):
+        q = g * depth
+        for parity in range(2):
+
+            @pl.when(side == parity)
+            def _():
+                away = depth - 1 - p if parity == 1 else p
+                sign = 1.0 if parity == 1 else -1.0
+                near, beyond = (q, q + 1) if parity == 1 else (q + 1, q)
+                if away == 0:
+                    one, two = halo[parity, near], halo[parity, beyond]
+                    lap = (16.0 * one - two) * (1.0 / 12.0)
+                    gz = (8.0 * one - two) * (sign / 12.0)
+                else:
+                    two = halo[parity, near]
+                    lap = two * (-1.0 / 12.0)
+                    gz = two * (-sign / 12.0)
+                tail_ref[g - (count - 2 * TAIL), p] += lap
+                rhs_ref[g, p] += own[12 * depth + p] * gz
+
+    @pl.loop(0, count - TAIL)
     def _(g):
         more = g + LAG < count
 
@@ -376,10 +412,18 @@
                 wloc[m] = wtmp[:, :, m * per : (m + 1) * per, :]
             wrecv[dev] = wloc[dev]
 
-        @pl.when(g == 12 + WEYL_STEPS)
+        @pl.when(g == jnp.where(lax.rem(grp, 2) == 0, SPREAD_EVEN, SPREAD_ODD))
         def _():
             for offset in range(1, members):
                 spread(peer(offset), dev).start()
+
+    for g in range(count - TAIL, count):
+        for p in range(depth):
+            without_far(g, p)
+    for g in range(count - 1, count - TAIL - 1, -1):
+        relayed(g)
+        for p in range(depth):
+            far_share(g, p)
 
     others = pl.ds(0, members - 1)
     remote(wrecv.at[others], wrecv.at[others], send_w, recv_w, (grp, dev)).wait_recv()

time: 83.5 us -> 82.6 us (0.989)
  no operation moved by 1% of the time
where the time goes in v5:
time: 82.6 us; the launch traced here: 81.9 us
  Pallas kernels  81.3 us (98%)
    pallas_call x1, Pallas kernels, per_device(): pl.pallas_call(functools.partial(kernel, groups, members), out_shape=(sha...  79.4 us
    pallas_call x1, Pallas kernels, per_device(): pl.pallas_call(functools.partial(finish, members), out_shape=(share(field...  1.85 us

profile of v5, /device:TPU:0, one launch (start us, length us, event | category | flops | bytes accessed | tf_op | source)
XLA Modules:
  0.0 81.9 jit_solution(10257262744088436132)
XLA Ops:
  0.6 79.4 %evolve.1 = (f32[24,2,128,128]{3,2,1,0:T(8,128)S(1)}, f32[8,2,2,16,128]{4,3,2,1,0:T(8,128)S(1)}, f32[4,2,128,128]{3,2,1,0:T(8,128)S(1)}, f32[24,4,8,128]{3,2,1,0:T(8,128)S(1)}) custom-call(f32[48,128,128]{2,1,0:T(8,128)} %bitcast.1, f32[24,24]{1,0:T(8,128)} %mix_hbm.1, f32[24,24]{1,0:T(8,128)} %lap_hbm.1), custom_call_target="tpu_custom_call" | custom-call | tf_op jit(solution)/shard_map/evolve/pallas_call | solution.py:503
  80.1 1.9 %finish.1 = (f32[24,2,128,128]{3,2,1,0:T(8,128)}, f32[2,16,16,128]{3,2,1,0:T(8,128)}) custom-call(f32[24,2,128,128]{3,2,1,0:T(8,128)S(1)} %get-tuple-element.6.part_ref, f32[8,2,2,16,128]{4,3,2,1,0:T(8,128)S(1)} %get-tuple-element.7.wrecv, f32[4,2,128,128]{3,2,1,0:T(8,128)S(1)} %get-tuple-element.8.tail_ref, f32[24,4,8,128]{3,2,1,0:T(8,128)S(1)} %get-tuple-element.9.coef_ref), custom_call_target="tpu_custom_call" | custom-call | tf_op jit(solution)/shard_map/finish/pallas_call | solution.py:547

commit v6 on v5

--- a/solution.py
+++ b/solution.py
@@ -7,12 +7,12 @@
 from jax.experimental.pallas import tpu as pltpu
 from jax.sharding import PartitionSpec as P
 
-AHEAD = 12
+AHEAD = 6
 LAG = 4
 WEYL_STEPS = 4
 SPREAD_EVEN = 16
 SPREAD_ODD = 20
-STRIP = 32
+STRIP = 16
 MIX = 64
 TAIL = 2
 HALVES = 2

time: 82.6 us -> 82.5 us (level)
  no operation moved by 1% of the time
where the time goes in v6:
time: 82.5 us; the launch traced here: 82.1 us
  Pallas kernels  81.4 us (99%)
    pallas_call x1, Pallas kernels, per_device(): pl.pallas_call(functools.partial(kernel, groups, members), out_shape=(sha...  79.6 us
    pallas_call x1, Pallas kernels, per_device(): pl.pallas_call(functools.partial(finish, members), out_shape=(share(field...  1.81 us

profile of v6, /device:TPU:0, one launch (start us, length us, event | category | flops | bytes accessed | tf_op | source)
XLA Modules:
  0.0 82.1 jit_solution(8484771001087207364)
XLA Ops:
  0.6 79.6 %evolve.1 = (f32[24,2,128,128]{3,2,1,0:T(8,128)S(1)}, f32[8,2,2,16,128]{4,3,2,1,0:T(8,128)S(1)}, f32[4,2,128,128]{3,2,1,0:T(8,128)S(1)}, f32[24,4,8,128]{3,2,1,0:T(8,128)S(1)}) custom-call(f32[48,128,128]{2,1,0:T(8,128)} %bitcast.1, f32[24,24]{1,0:T(8,128)} %mix_hbm.1, f32[24,24]{1,0:T(8,128)} %lap_hbm.1), custom_call_target="tpu_custom_call" | custom-call | tf_op jit(solution)/shard_map/evolve/pallas_call | solution.py:503
  80.2 1.8 %finish.1 = (f32[24,2,128,128]{3,2,1,0:T(8,128)}, f32[2,16,16,128]{3,2,1,0:T(8,128)}) custom-call(f32[24,2,128,128]{3,2,1,0:T(8,128)S(1)} %get-tuple-element.6.part_ref, f32[8,2,2,16,128]{4,3,2,1,0:T(8,128)S(1)} %get-tuple-element.7.wrecv, f32[4,2,128,128]{3,2,1,0:T(8,128)S(1)} %get-tuple-element.8.tail_ref, f32[24,4,8,128]{3,2,1,0:T(8,128)S(1)} %get-tuple-element.9.coef_ref), custom_call_target="tpu_custom_call" | custom-call | tf_op jit(solution)/shard_map/finish/pallas_call | solution.py:547

commit v7 on v6

--- a/solution.py
+++ b/solution.py
@@ -463,7 +463,7 @@
     for source in range(members):
         layers = pl.ds(source * depth, depth)
         blocks.append(
-            pltpu.make_async_copy(wrecv.at[source], weyl_ref.at[:, layers], weyl_sem.at[source])
+            pltpu.make_async_copy(wrecv.at[source], weyl_ref.at[:, layers], weyl_sem)
         )
     for block in blocks:
         block.start()
@@ -486,8 +486,7 @@
                 whole[c, p, part, :] = value
         pltpu.make_async_copy(whole.at[:, p, strip], rhs_ref.at[:, p, strip], rhs_sem).start()
 
-    for block in blocks:
-        block.wait()
+    pltpu.make_async_copy(weyl_ref, weyl_ref, weyl_sem).wait()
     pltpu.make_async_copy(whole, rhs_ref, rhs_sem).wait()
 
 
@@ -549,7 +548,7 @@
         out_shape=(share(fields.shape), share((2, depth * members, per, width))),
         in_specs=[in_vmem] * 4,
         out_specs=(in_hbm,) * 2,
-        scratch_shapes=[vmem((count, depth) + plane), dma, dma((members,))],
+        scratch_shapes=[vmem((count, depth) + plane), dma, dma],
         compiler_params=pltpu.CompilerParams(vmem_limit_bytes=8 * 1024 * 1024),
         name="finish",
     )(*pieces)

time: 82.5 us -> 82.4 us (level)
  no operation moved by 1% of the time
where the time goes in v7:
time: 82.4 us; the launch traced here: 82 us
  Pallas kernels  81.4 us (99%)
    pallas_call x1, Pallas kernels, per_device(): pl.pallas_call(functools.partial(kernel, groups, members), out_shape=(sha...  79.6 us
    pallas_call x1, Pallas kernels, per_device(): pl.pallas_call(functools.partial(finish, members), out_shape=(share(field...  1.75 us

profile of v7, /device:TPU:0, one launch (start us, length us, event | category | flops | bytes accessed | tf_op | source)
XLA Modules:
  0.0 82.0 jit_solution(18181571951302748068)
XLA Ops:
  0.6 79.6 %evolve.1 = (f32[24,2,128,128]{3,2,1,0:T(8,128)S(1)}, f32[8,2,2,16,128]{4,3,2,1,0:T(8,128)S(1)}, f32[4,2,128,128]{3,2,1,0:T(8,128)S(1)}, f32[24,4,8,128]{3,2,1,0:T(8,128)S(1)}) custom-call(f32[48,128,128]{2,1,0:T(8,128)} %bitcast.1, f32[24,24]{1,0:T(8,128)} %mix_hbm.1, f32[24,24]{1,0:T(8,128)} %lap_hbm.1), custom_call_target="tpu_custom_call" | custom-call | tf_op jit(solution)/shard_map/evolve/pallas_call | solution.py:502
  80.2 1.8 %finish.1 = (f32[24,2,128,128]{3,2,1,0:T(8,128)}, f32[2,16,16,128]{3,2,1,0:T(8,128)}) custom-call(f32[24,2,128,128]{3,2,1,0:T(8,128)S(1)} %get-tuple-element.6.part_ref, f32[8,2,2,16,128]{4,3,2,1,0:T(8,128)S(1)} %get-tuple-element.7.wrecv, f32[4,2,128,128]{3,2,1,0:T(8,128)S(1)} %get-tuple-element.8.tail_ref, f32[24,4,8,128]{3,2,1,0:T(8,128)S(1)} %get-tuple-element.9.coef_ref), custom_call_target="tpu_custom_call" | custom-call | tf_op jit(solution)/shard_map/finish/pallas_call | solution.py:546
